TPU v7x, 32 devices: a whole 2x2x4 slice. The times are simulated.
32 devices in a mesh: tm: 8 (over y, x, core), chan: 4 (over z).
Axes of the slice: x: 2, y: 2, z: 4, core: 2. Of those that a mesh axis runs over, the one named last changes fastest.
Arguments:
- auxiliary: float32 [512, 262144], P('chan', 'tm'), may hold values from -30 to 30
- proofs: float32 [64, 262144], P('chan', 'tm'), may hold values from -12 to 12
Outputs:
- coherence: float32 [512, 64, 4096], P('chan', None, 'tm')
All inputs are finite; a program needn't handle non-finite values.
Results may differ from a plain program's by a relative error of at most 0.00076.
Values may be sent and summed in bfloat16 or wider, within the bound.
A program may use at most 192 MiB of HBM per device.

v0:
```python
import math
import jax
import jax.numpy as jnp
from jax import lax
from jax.sharding import PartitionSpec as P

SEG_LEN = 8192
FACTOR = 64
STRIDE = 4096
BINS = 4096


def shifted(value, axis, by):
    peers = lax.axis_size(axis)
    pairs = [(i, i + by) for i in range(peers) if 0 <= i + by < peers]
    return lax.ppermute(value, axis, pairs)


def angle_table(left_count, right_count, modulus):
    left_index = jnp.arange(left_count, dtype=jnp.int32)
    right_index = jnp.arange(right_count, dtype=jnp.int32)
    product = left_index[:, None] * right_index[None, :] % modulus
    return 2.0 * math.pi / modulus * product.astype(jnp.float32)


def transform_block(windowed):
    row_count = windowed.shape[0]
    second = SEG_LEN // FACTOR
    highest = lax.Precision.HIGHEST
    angle_first = angle_table(FACTOR, FACTOR, FACTOR)
    angle_twist = angle_table(FACTOR, second, SEG_LEN)
    angle_second = angle_table(second, second // 2, second)
    cos_twist = jnp.cos(angle_twist)
    sin_twist = jnp.sin(angle_twist)
    cos_second = jnp.cos(angle_second)
    sin_second = jnp.sin(angle_second)
    shaped = windowed.reshape(row_count, FACTOR, second)
    real_one = jnp.einsum("rpq,pk->rkq", shaped, jnp.cos(angle_first), precision=highest)
    imag_one = -jnp.einsum("rpq,pk->rkq", shaped, jnp.sin(angle_first), precision=highest)
    real_two = real_one * cos_twist + imag_one * sin_twist
    imag_two = imag_one * cos_twist - real_one * sin_twist
    real_out = jnp.einsum("rkq,qm->rmk", real_two, cos_second, precision=highest) + jnp.einsum(
        "rkq,qm->rmk", imag_two, sin_second, precision=highest
    )
    imag_out = jnp.einsum("rkq,qm->rmk", imag_two, cos_second, precision=highest) - jnp.einsum(
        "rkq,qm->rmk", real_two, sin_second, precision=highest
    )
    return (real_out.reshape(row_count, BINS), imag_out.reshape(row_count, BINS))


def transform(windowed):
    row_count = windowed.shape[0]
    block_rows = math.gcd(row_count, 64)
    blocks = windowed.reshape(row_count // block_rows, block_rows, SEG_LEN)
    real_out, imag_out = lax.map(transform_block, blocks)
    return (real_out.reshape(row_count, BINS), imag_out.reshape(row_count, BINS))


def segments_of(signal, seg_count):
    channels = signal.shape[0]
    blocks = signal.reshape(channels, seg_count + 1, STRIDE)
    segments = jnp.concatenate([blocks[:, :-1], blocks[:, 1:]], axis=2)
    position = jnp.arange(SEG_LEN, dtype=jnp.float32)
    window = 0.5 - 0.5 * jnp.cos(2.0 * math.pi * position / SEG_LEN)
    return (segments * window).reshape(channels * seg_count, SEG_LEN)


def channel_totals(local_sums):
    return lax.psum((local_sums[0], local_sums[1]), "tm")


def coherence_block(aux_moved, aux_power, wit_piece):
    left_real = jnp.concatenate([aux_moved[0], aux_moved[1]], axis=1)
    left_imag = jnp.concatenate([aux_moved[1], -aux_moved[0]], axis=1)
    right_side = jnp.concatenate([wit_piece[0], wit_piece[1]], axis=1)
    cross_real = jnp.einsum(
        "csf,wsf->cwf", left_real, right_side, preferred_element_type=jnp.float32
    )
    cross_imag = jnp.einsum(
        "csf,wsf->cwf", left_imag, right_side, preferred_element_type=jnp.float32
    )
    wit_float = wit_piece.astype(jnp.float32)
    wit_power = jnp.sum(wit_float * wit_float, axis=(0, 2))
    return (cross_real * cross_real + cross_imag * cross_imag) / (
        (aux_power[:, None, :] + 1e-06) * (wit_power[None, :, :] + 1e-06)
    )


def per_device(auxiliary, proofs):
    aux_rows = auxiliary.shape[0]
    seg_count = auxiliary.shape[1] // STRIDE
    tm_size = lax.axis_size("tm")
    next_aux, next_wit = shifted((auxiliary[:, :STRIDE], proofs[:, :STRIDE]), "tm", -1)
    signal = jnp.concatenate(
        [
            jnp.concatenate([auxiliary, next_aux], axis=1),
            jnp.concatenate([proofs, next_wit], axis=1),
        ],
        axis=0,
    )
    channels = signal.shape[0]
    local_sums = (jnp.sum(auxiliary, axis=1), jnp.sum(proofs, axis=1))
    total_samples = auxiliary.shape[1] * tm_size
    real_part, imag_part = transform(segments_of(signal, seg_count))
    totals = channel_totals(local_sums)
    channel_means = jnp.concatenate(totals) / total_samples
    bin_index = jnp.arange(BINS, dtype=jnp.int32)
    offset_table = jnp.where(
        bin_index == 0, -0.5 * SEG_LEN, jnp.where(bin_index == 1, 0.25 * SEG_LEN, 0.0)
    ).astype(jnp.float32)
    real_part = real_part + jnp.repeat(channel_means, seg_count)[:, None] * offset_table[None, :]
    spectra = (
        jnp.stack([real_part, imag_part]).astype(jnp.bfloat16).reshape(2, channels, seg_count, BINS)
    )
    aux_spec = spectra[:, :aux_rows]
    wit_spec = spectra[:, aux_rows:]
    aux_moved, wit_moved = (
        lax.all_to_all(aux_spec, "tm", split_axis=3, concat_axis=2, tiled=True),
        lax.all_to_all(wit_spec, "tm", split_axis=3, concat_axis=2, tiled=True),
    )
    kept_segments = seg_count * tm_size - 1
    aux_moved = aux_moved[:, :, :kept_segments]
    wit_moved = wit_moved[:, :, :kept_segments]
    aux_float = aux_moved.astype(jnp.float32)
    aux_power = jnp.sum(aux_float * aux_float, axis=(0, 2))
    return coherence_block(
        aux_moved, aux_power, lax.all_gather(wit_moved, "chan", axis=1, tiled=True)
    )


def solution(mesh):
    return jax.shard_map(
        per_device,
        mesh=mesh,
        in_specs=(P("chan", "tm"), P("chan", "tm")),
        out_specs=P("chan", None, "tm"),
        check_vma=False,
    )
```

profile of v0, /device:TPU:0, one launch (start us, length us, event | category | flops | bytes accessed | tf_op | source)
XLA Modules:
  0.0 1519.9 jit_solution(11121710718804022927)
XLA Ops:
  11.1 6.6 reduce_sum.36
  19.4 28.3 %all-reduce = (f32[16]{0:T(128)S(1)}, f32[128]{0:T(128)S(1)}) all-reduce(f32[16]{0:T(128)S(1)} %reduce_sum.37, f32[128]{0:T(128)S(1)} %reduce_sum.36), channel_id=1, replica_groups=mesh['tm'=8,'chan'=4] {'tm'}, use_global_device_ids=true, to_apply=%region_5.6 | all-reduce | flops 144 | bytes 1152 | tf_op jit(solution)/shard_map/psum | solution.py:69
  47.8 19.2 %maximum_maximum_fusion = f32[144,36864]{1,0:T(8,128)} fusion(f32[16,4096]{1,0:T(8,128)S(1)} %collective-permute-done.1, f32[16,32768]{1,0:T(8,128)S(1)} %copy-done.6, f32[128,4096]{1,0:T(8,128)} %collective-permute-done, f32[128,32768]{1,0:T(8,128)} %param.4), kind=kLoop, calls=%fused_computation.83 | loop fusion | flops 15925248 | bytes 42467328 | tf_op jit(solution)/shard_map/concatenate | solution.py:94
  67.0 23.5 %reshape.121 = f32[144,9,4096]{2,1,0:T(8,128)} reshape(f32[144,36864]{1,0:T(8,128)} %maximum_maximum_fusion) | data formatting | bytes 42467328 | tf_op jit(solution)/shard_map/reshape | solution.py:61
  90.5 32.4 %fusion.86 = (f32[144,8,4096]{2,1,0:T(8,128)}, f32[144,8,4096]{2,1,0:T(8,128)}) fusion(f32[144,9,4096]{2,1,0:T(8,128)} %reshape.121), kind=kLoop, calls=%fused_computation.109 | loop fusion | bytes 75497472 | tf_op jit(solution)/shard_map/slice | solution.py:62
  122.9 24.7 %maximum_multiply_fusion = f32[18,64,8192]{2,1,0:T(8,128)} fusion(f32[18,64,4096]{2,1,0:T(8,128)} %bitcast.103, f32[18,64,4096]{2,1,0:T(8,128)} %bitcast.102, f32[8192]{0:T(1024)S(1)} %multiply_subtract_fusion.3), kind=kLoop, calls=%fused_computation.80 | loop fusion | flops 18874368 | bytes 75530240 | tf_op jit(solution)/shard_map/mul | solution.py:65
  147.7 764.7 %while.15 = (s32[]{:T(128)}, f32[18,64,4096]{2,1,0:T(8,128)}, bf16[18,64,4096]{2,1,0:T(8,128)(2,1)}, f32[18,64,8192]{2,1,0:T(8,128)}, s32[]{:T(128)}) while((s32[]{:T(128)}, f32[18,64,4096]{2,1,0:T(8,128)}, bf16[18,64,4096]{2,1,0:T(8,128)(2,1)}, f32[18,64,8192]{2,1,0:T(8,128)}, s32[]{:T(128)}) %tuple.35), condition=%wide.region_1.0_spmd, body=%wide.region_0.0_spmd.sunk | while | flops 2425782272 | bytes 56426632 | solution.py:55
  182.6 7.8 fusion.122
  190.4 9.2 add_bitcast_fusion.2
  224.2 7.8 fusion.122
  232.0 9.2 add_bitcast_fusion.2
  265.8 7.8 fusion.122
  273.6 9.2 add_bitcast_fusion.2
  307.5 7.8 fusion.122
  315.3 9.2 add_bitcast_fusion.2
  349.2 7.8 fusion.122
  357.0 9.2 add_bitcast_fusion.2
  390.8 7.8 fusion.122
  398.6 9.2 add_bitcast_fusion.2
  432.5 7.8 fusion.122
  440.3 9.2 add_bitcast_fusion.2
  466.3 6.3 subtract_bitcast_fusion.2
  474.1 7.8 fusion.122
  482.0 9.2 add_bitcast_fusion.2
  515.8 7.8 fusion.122
  523.6 9.2 add_bitcast_fusion.2
  557.5 7.8 fusion.122
  565.3 9.2 add_bitcast_fusion.2
  599.2 7.8 fusion.122
  607.0 9.2 add_bitcast_fusion.2
  640.8 7.8 fusion.122
  648.6 9.2 add_bitcast_fusion.2
  682.5 7.8 fusion.122
  690.3 9.2 add_bitcast_fusion.2
  716.3 6.3 subtract_bitcast_fusion.2
  724.1 7.8 fusion.122
  732.0 9.2 add_bitcast_fusion.2
  765.8 7.8 fusion.122
  773.6 9.2 add_bitcast_fusion.2
  807.5 7.8 fusion.122
  815.3 9.2 add_bitcast_fusion.2
  849.2 7.8 fusion.122
  857.0 9.2 add_bitcast_fusion.2
  890.9 7.8 fusion.122
  898.7 9.2 add_bitcast_fusion.2
  912.4 8.4 add_convert_fusion
  924.6 13.7 copy.29
  938.3 18.8 %reshape.127 = bf16[8,2,65536]{2,1,0:T(2,128)(2,1)S(1)} reshape(bf16[4096,2,8,16]{3,2,1,0:T(8,128)(2,1)} %bitcast.104) | data formatting | bytes 4194304
  957.2 31.7 %all_to_all.36 = bf16[8,2,65536]{2,1,0:T(2,128)(2,1)} all-to-all(bf16[8,2,65536]{2,1,0:T(2,128)(2,1)S(1)} %reshape.127), channel_id=1, replica_groups=mesh['tm'=8,'chan'=4] {'tm'}, dimensions={0} | all-to-all | bytes 4194304 | tf_op jit(solution)/shard_map/all_to_all | solution.py:119
  988.8 13.9 reshape.128
  1002.8 17.5 %copy.31 = bf16[2,16,8,8,512]{4,3,2,1,0:T(8,128)(2,1)S(1)} copy(bf16[2,16,8,8,512]{1,3,0,4,2:T(8,128)(2,1)} %bitcast.105) | data formatting | bytes 4194304 | tf_op jit(solution)/shard_map/all_to_all | solution.py:119
  1025.2 15.3 %pad_maximum_fusion = bf16[2,128,8,4096]{3,2,1,0:T(8,128)(2,1)} fusion(bf16[1,144,8,4096]{3,2,1,0:T(8,128)(2,1)} %bitcast.108, bf16[1,144,8,4096]{3,2,1,0:T(8,128)(2,1)} %copy-done.2), kind=kLoop, calls=%fused_computation.85 | loop fusion | flops 8388608 | bytes 35651584 | tf_op jit(solution)/shard_map/stack | solution.py:113
  1040.5 24.3 %copy.33 = bf16[2,128,8,4096]{1,2,0,3:T(8,128)(2,1)} copy(bf16[2,128,8,4096]{3,2,1,0:T(8,128)(2,1)} %pad_maximum_fusion) | data formatting | bytes 33554432 | tf_op jit(solution)/shard_map/slice | solution.py:115
  1070.7 240.2 %all-gather.2.cloned.1.call-done = bf16[2,64,63,512]{2,1,3,0:T(8,128)(2,1)} async-done(((bf16[2,16,63,512]{2,1,3,0:T(8,128)(2,1)}), bf16[2,64,63,512]{2,1,3,0:T(8,128)(2,1)}) %all-gather.2.cloned.1.call-update) | async-done | bytes 8257552 | tf_op jit(solution)/shard_map/all_gather | solution.py:127
  1311.0 8.3 multiply_reduce_fusion
  1321.7 7.2 slice_bitcast_fusion.1
  1328.9 25.1 %copy.35 = bf16[2,128,8,8,512]{4,3,2,1,0:T(8,128)(2,1)} copy(bf16[2,128,8,8,512]{1,3,0,4,2:T(8,128)(2,1)} %bitcast.20) | data formatting | bytes 33554432 | tf_op jit(solution)/shard_map/all_to_all | solution.py:118
  1354.1 7.5 multiply_reduce_fusion.1
  1371.0 26.8 %copy.44 = bf16[1,128,63,512]{2,1,3,0:T(8,128)(2,1)} copy(bf16[1,128,63,512]{3,2,1,0:T(8,128)(2,1)} %get-tuple-element.101) | data formatting | bytes 16515072
  1397.8 14.2 bitcast_negate_fusion
  1412.0 26.7 %copy.45 = bf16[1,128,63,512]{2,1,3,0:T(8,128)(2,1)} copy(bf16[1,128,63,512]{3,2,1,0:T(8,128)(2,1)} %get-tuple-element.102) | data formatting | bytes 16515072
  1438.6 26.9 %fusion.74 = f32[512,64,128]{2,1,0:T(8,128)} fusion(bf16[128,63,512]{1,0,2:T(8,128)(2,1)} %bitcast.106, bf16[128,63,512]{1,0,2:T(8,128)(2,1)} %bitcast.101, bf16[64,63,512]{1,0,2:T(8,128)(2,1)} %get-tuple-element.100, bf16[64,63,512]{1,0,2:T(8,128)(2,1)} %get-tuple-element.99), kind=kOutput, calls=%fused_computation.86 | convolution fusion | flops 1106509824 | bytes 41549824 | tf_op jit(solution)/shard_map/csf,wsf->cwf/dot_general | solution.py:76
  1465.5 29.8 %bitcast_divide_fusion = f32[128,64,512]{0,1,2:T(8,128)} fusion(f32[512,64,128]{2,1,0:T(8,128)} %fusion.74, bf16[128,63,512]{1,0,2:T(8,128)(2,1)} %bitcast_negate_fusion, bf16[128,63,512]{1,0,2:T(8,128)(2,1)} %bitcast.107, f32[64,512]{0,1:T(8,128)S(1)} %broadcast_add_fusion, f32[128,512]{0,1:T(8,128)S(1)} %copy.38, ...), kind=kOutput, calls=%fused_computation.94 | convolution fusion | flops 1127481344 | bytes 58720256 | tf_op jit(solution)/shard_map/csf,wsf->cwf/dot_general | solution.py:79
  1495.4 17.5 %copy.39 = f32[128,64,512]{2,1,0:T(8,128)} copy(f32[128,64,512]{0,1,2:T(8,128)} %bitcast_divide_fusion) | data formatting | bytes 33554432 | tf_op jit(solution)/shard_map/div | solution.py:84
  (300 shorter events, 462.5 us)
Async XLA Ops:
  6.5 1304.4 %all-gather.2.cloned.1.call-start = ((), (), s32[]{:S(2)}) async-start(), calls=%async_computation.2 | async-start | bytes 20971520 | tf_op jit(solution)/shard_map/all_gather | solution.py:127
  9.6 8.0 copy-start.6
  9.7 38.2 %collective-permute-start = (f32[128,4096]{1,0:T(8,128)}, f32[128,4096]{1,0:T(8,128)}, u32[]{:S(2)}, u32[]{:S(2)}) collective-permute-start(f32[128,4096]{1,0:T(8,128)} %slice.40), channel_id=1, source_target_pairs={{4,0},{8,4},{12,8},{16,12},{20,16},{24,20},{28,24},{5,1},{9,5},{13... | collective-permute-start | bytes 6291464 | tf_op jit(solution)/shard_map/ppermute | solution.py:16
  18.1 29.8 %collective-permute-start.1 = (f32[16,4096]{1,0:T(8,128)S(1)}, f32[16,4096]{1,0:T(8,128)S(1)}, u32[]{:S(2)}, u32[]{:S(2)}) collective-permute-start(f32[16,4096]{1,0:T(8,128)S(1)} %slice.41), channel_id=1, source_target_pairs={{4,0},{8,4},{12,8},{16,12},{20,16},{24,20},{28,24},{5,1},{9,5},{13... | collective-permute-start | bytes 786440 | tf_op jit(solution)/shard_map/ppermute | solution.py:16
  168.5 6.2 copy-start
  182.6 19.2 %copy-start.4 = (bf16[1,64,4096]{2,1,0:T(8,128)(2,1)S(1)}, bf16[1,64,4096]{2,1,0:T(8,128)(2,1)}, u32[]{:S(2)}) copy-start(bf16[1,64,4096]{2,1,0:T(8,128)(2,1)} %broadcast_in_dim.51) | copy-start | bytes 1572868 | tf_op jit(solution)/shard_map/while
  210.1 6.2 copy-start
  224.2 19.2 %copy-start.4 = (bf16[1,64,4096]{2,1,0:T(8,128)(2,1)S(1)}, bf16[1,64,4096]{2,1,0:T(8,128)(2,1)}, u32[]{:S(2)}) copy-start(bf16[1,64,4096]{2,1,0:T(8,128)(2,1)} %broadcast_in_dim.51) | copy-start | bytes 1572868 | tf_op jit(solution)/shard_map/while
  251.7 6.2 copy-start
  265.8 19.2 %copy-start.4 = (bf16[1,64,4096]{2,1,0:T(8,128)(2,1)S(1)}, bf16[1,64,4096]{2,1,0:T(8,128)(2,1)}, u32[]{:S(2)}) copy-start(bf16[1,64,4096]{2,1,0:T(8,128)(2,1)} %broadcast_in_dim.51) | copy-start | bytes 1572868 | tf_op jit(solution)/shard_map/while
  293.4 6.2 copy-start
  307.5 19.2 %copy-start.4 = (bf16[1,64,4096]{2,1,0:T(8,128)(2,1)S(1)}, bf16[1,64,4096]{2,1,0:T(8,128)(2,1)}, u32[]{:S(2)}) copy-start(bf16[1,64,4096]{2,1,0:T(8,128)(2,1)} %broadcast_in_dim.51) | copy-start | bytes 1572868 | tf_op jit(solution)/shard_map/while
  335.1 6.2 copy-start
  349.2 19.2 %copy-start.4 = (bf16[1,64,4096]{2,1,0:T(8,128)(2,1)S(1)}, bf16[1,64,4096]{2,1,0:T(8,128)(2,1)}, u32[]{:S(2)}) copy-start(bf16[1,64,4096]{2,1,0:T(8,128)(2,1)} %broadcast_in_dim.51) | copy-start | bytes 1572868 | tf_op jit(solution)/shard_map/while
  376.7 6.2 copy-start
  390.8 19.2 %copy-start.4 = (bf16[1,64,4096]{2,1,0:T(8,128)(2,1)S(1)}, bf16[1,64,4096]{2,1,0:T(8,128)(2,1)}, u32[]{:S(2)}) copy-start(bf16[1,64,4096]{2,1,0:T(8,128)(2,1)} %broadcast_in_dim.51) | copy-start | bytes 1572868 | tf_op jit(solution)/shard_map/while
  418.4 6.2 copy-start
  432.5 19.2 %copy-start.4 = (bf16[1,64,4096]{2,1,0:T(8,128)(2,1)S(1)}, bf16[1,64,4096]{2,1,0:T(8,128)(2,1)}, u32[]{:S(2)}) copy-start(bf16[1,64,4096]{2,1,0:T(8,128)(2,1)} %broadcast_in_dim.51) | copy-start | bytes 1572868 | tf_op jit(solution)/shard_map/while
  460.0 6.2 copy-start
  474.1 19.2 %copy-start.4 = (bf16[1,64,4096]{2,1,0:T(8,128)(2,1)S(1)}, bf16[1,64,4096]{2,1,0:T(8,128)(2,1)}, u32[]{:S(2)}) copy-start(bf16[1,64,4096]{2,1,0:T(8,128)(2,1)} %broadcast_in_dim.51) | copy-start | bytes 1572868 | tf_op jit(solution)/shard_map/while
  501.7 6.2 copy-start
  515.8 19.2 %copy-start.4 = (bf16[1,64,4096]{2,1,0:T(8,128)(2,1)S(1)}, bf16[1,64,4096]{2,1,0:T(8,128)(2,1)}, u32[]{:S(2)}) copy-start(bf16[1,64,4096]{2,1,0:T(8,128)(2,1)} %broadcast_in_dim.51) | copy-start | bytes 1572868 | tf_op jit(solution)/shard_map/while
  543.4 6.2 copy-start
  557.5 19.2 %copy-start.4 = (bf16[1,64,4096]{2,1,0:T(8,128)(2,1)S(1)}, bf16[1,64,4096]{2,1,0:T(8,128)(2,1)}, u32[]{:S(2)}) copy-start(bf16[1,64,4096]{2,1,0:T(8,128)(2,1)} %broadcast_in_dim.51) | copy-start | bytes 1572868 | tf_op jit(solution)/shard_map/while
  585.1 6.2 copy-start
  599.2 19.2 %copy-start.4 = (bf16[1,64,4096]{2,1,0:T(8,128)(2,1)S(1)}, bf16[1,64,4096]{2,1,0:T(8,128)(2,1)}, u32[]{:S(2)}) copy-start(bf16[1,64,4096]{2,1,0:T(8,128)(2,1)} %broadcast_in_dim.51) | copy-start | bytes 1572868 | tf_op jit(solution)/shard_map/while
  626.7 6.2 copy-start
  640.8 19.2 %copy-start.4 = (bf16[1,64,4096]{2,1,0:T(8,128)(2,1)S(1)}, bf16[1,64,4096]{2,1,0:T(8,128)(2,1)}, u32[]{:S(2)}) copy-start(bf16[1,64,4096]{2,1,0:T(8,128)(2,1)} %broadcast_in_dim.51) | copy-start | bytes 1572868 | tf_op jit(solution)/shard_map/while
  668.4 6.2 copy-start
  682.5 19.2 %copy-start.4 = (bf16[1,64,4096]{2,1,0:T(8,128)(2,1)S(1)}, bf16[1,64,4096]{2,1,0:T(8,128)(2,1)}, u32[]{:S(2)}) copy-start(bf16[1,64,4096]{2,1,0:T(8,128)(2,1)} %broadcast_in_dim.51) | copy-start | bytes 1572868 | tf_op jit(solution)/shard_map/while
  710.1 6.2 copy-start
  724.1 19.2 %copy-start.4 = (bf16[1,64,4096]{2,1,0:T(8,128)(2,1)S(1)}, bf16[1,64,4096]{2,1,0:T(8,128)(2,1)}, u32[]{:S(2)}) copy-start(bf16[1,64,4096]{2,1,0:T(8,128)(2,1)} %broadcast_in_dim.51) | copy-start | bytes 1572868 | tf_op jit(solution)/shard_map/while
  751.7 6.2 copy-start
  765.8 19.2 %copy-start.4 = (bf16[1,64,4096]{2,1,0:T(8,128)(2,1)S(1)}, bf16[1,64,4096]{2,1,0:T(8,128)(2,1)}, u32[]{:S(2)}) copy-start(bf16[1,64,4096]{2,1,0:T(8,128)(2,1)} %broadcast_in_dim.51) | copy-start | bytes 1572868 | tf_op jit(solution)/shard_map/while
  793.4 6.2 copy-start
  807.5 19.2 %copy-start.4 = (bf16[1,64,4096]{2,1,0:T(8,128)(2,1)S(1)}, bf16[1,64,4096]{2,1,0:T(8,128)(2,1)}, u32[]{:S(2)}) copy-start(bf16[1,64,4096]{2,1,0:T(8,128)(2,1)} %broadcast_in_dim.51) | copy-start | bytes 1572868 | tf_op jit(solution)/shard_map/while
  835.1 6.2 copy-start
  849.2 19.2 %copy-start.4 = (bf16[1,64,4096]{2,1,0:T(8,128)(2,1)S(1)}, bf16[1,64,4096]{2,1,0:T(8,128)(2,1)}, u32[]{:S(2)}) copy-start(bf16[1,64,4096]{2,1,0:T(8,128)(2,1)} %broadcast_in_dim.51) | copy-start | bytes 1572868 | tf_op jit(solution)/shard_map/while
  876.8 6.2 copy-start
  890.9 19.2 %copy-start.4 = (bf16[1,64,4096]{2,1,0:T(8,128)(2,1)S(1)}, bf16[1,64,4096]{2,1,0:T(8,128)(2,1)}, u32[]{:S(2)}) copy-start(bf16[1,64,4096]{2,1,0:T(8,128)(2,1)} %broadcast_in_dim.51) | copy-start | bytes 1572868 | tf_op jit(solution)/shard_map/while
  912.4 12.0 copy-start.5
  920.8 3.6 copy-start.2
  1064.8 264.1 %all-to-all-start.1 = ((bf16[2,128,8,4096]{1,2,0,3:T(8,128)(2,1)}), bf16[2,128,8,4096]{1,2,0,3:T(8,128)(2,1)}, u32[]{:S(2)}, u32[]{:S(2)}) async-start(bf16[2,128,8,4096]{1,2,0,3:T(8,128)(2,1)} %copy.33), calls=%async_computation.1 | async-start | bytes 33554432 | tf_op jit(solution)/shard_map/all_to_all | solution.py:118
  1311.0 10.7 copy-start.3
  1354.1 10.7 copy-start.1
Sparse Core Ops, SparseCore 0:
  1025.3 285.5 all-gather.1
where the time goes:
time: 1530 us; the launch traced here: 1520 us
  matrix products  663 us (43%)
  local copies, waits for them, and re-layouts  411 us (27%)
  waiting for transfers between devices  240 us (16%)
  other arithmetic  108 us (7%)
  blocking collectives  59.9 us (4%)
  loops' own time  15.9 us (1%)
    all_gather x1, waiting for transfers between devices, per_device(): lax.all_gather(wit_moved, 'chan', axis=1, tiled=True)  240 us
    dot_general x18, matrix products, transform_block(): jnp.einsum('rkq,qm->rmk', real_two, cos_second, precision=highest)  166 us
    dot_general x18, matrix products, transform_block(): jnp.einsum('rkq,qm->rmk', imag_two, sin_second, precision=highest)  141 us
    dot_general x18, matrix products, transform_block(): jnp.einsum('rkq,qm->rmk', real_two, sin_second, precision=highest)  113 us
    dot_general x18, matrix products, transform_block(): jnp.einsum('rkq,qm->rmk', imag_two, cos_second, precision=highest)  112 us
    unnamed x15, local copies, waits for them, and re-layouts  100 us
    broadcast_in_dim x36, local copies, waits for them, and re-layouts, transform(): real_out, imag_out = lax.map(transform_block, blocks)  67.4 us
    while x108, local copies, waits for them, and re-layouts  38.3 us
  transfers between devices with their start and end apart: 4, of which 1 were waited for; matrix products, arithmetic and copies ran while one was open for 4% of the time, Pallas kernels for 0%

commit v1 on v0

--- a/solution.py
+++ b/solution.py
@@ -8,6 +8,11 @@
 FACTOR = 64
 STRIDE = 4096
 BINS = 4096
+
+
+def cover_trees(payload):
+    latest = lax.all_gather(payload, "chan")
+    return jnp.concatenate(latest, axis=1)
 
 
 def shifted(value, axis, by):
@@ -123,9 +128,7 @@
     wit_moved = wit_moved[:, :, :kept_segments]
     aux_float = aux_moved.astype(jnp.float32)
     aux_power = jnp.sum(aux_float * aux_float, axis=(0, 2))
-    return coherence_block(
-        aux_moved, aux_power, lax.all_gather(wit_moved, "chan", axis=1, tiled=True)
-    )
+    return coherence_block(aux_moved, aux_power, cover_trees(wit_moved))
 
 
 def solution(mesh):

time: 1530 us -> 1440 us (0.941)
  waiting for transfers between devices: 240 us -> 149 us
  local copies, waits for them, and re-layouts: 411 us -> 461 us
  blocking collectives: 59.9 us -> 27.3 us
    all_gather x1, waiting for transfers between devices: 240 us -> 149 us  [cover_trees(): latest = lax.all_gather(payload, 'chan')]
    slice x0 -> x4, local copies, waits for them, and re-layouts: none -> 38.2 us  [the longest x3 36.7 us: coherence_block(): right_side = jnp.concatenate([wit_piece[0], wit_piece[1]], axis=1)]
    all_to_all x1 -> x0, blocking collectives: 31.7 us -> none  [per_device(): lax.all_to_all(wit_spec, 'tm', split_axis=3, concat_axis=2, tiled=True)]
    dynamic_update_slice x36, local copies, waits for them, and re-layouts: 34.4 us -> 53.2 us  [transform(): real_out, imag_out = lax.map(transform_block, blocks)]
    unnamed x15 -> x18, local copies, waits for them, and re-layouts: 100 us -> 92.7 us
    while x108 -> x72, local copies, waits for them, and re-layouts: 38.3 us -> 38.1 us
  transfers between devices with their start and end apart: 4 -> 5, of which waited for: 1 -> 1; matrix products, arithmetic and copies ran while one was open for 4% -> 8% of each run, Pallas kernels for 0% -> 0%
where the time goes in v1:
time: 1440 us; the launch traced here: 1430 us
  matrix products  661 us (46%)
  local copies, waits for them, and re-layouts  461 us (32%)
  waiting for transfers between devices  149 us (10%)
  other arithmetic  101 us (7%)
  blocking collectives  27.3 us (2%)
    dot_general x18, matrix products, transform_block(): jnp.einsum('rkq,qm->rmk', real_two, cos_second, precision=highest)  165 us
    all_gather x1, waiting for transfers between devices, cover_trees(): latest = lax.all_gather(payload, 'chan')  149 us
    dot_general x18, matrix products, transform_block(): jnp.einsum('rkq,qm->rmk', imag_two, sin_second, precision=highest)  140 us
    dot_general x18, matrix products, transform_block(): jnp.einsum('rkq,qm->rmk', real_two, sin_second, precision=highest)  113 us
    dot_general x18, matrix products, transform_block(): jnp.einsum('rkq,qm->rmk', imag_two, cos_second, precision=highest)  112 us
    unnamed x18, local copies, waits for them, and re-layouts  92.7 us
    broadcast_in_dim x36, local copies, waits for them, and re-layouts, transform(): real_out, imag_out = lax.map(transform_block, blocks)  68.1 us
    dynamic_update_slice x36, local copies, waits for them, and re-layouts, transform(): real_out, imag_out = lax.map(transform_block, blocks)  53.2 us
  transfers between devices with their start and end apart: 5, of which 1 were waited for; matrix products, arithmetic and copies ran while one was open for 8% of the time, Pallas kernels for 0%

profile of v1, /device:TPU:0, one launch (start us, length us, event | category | flops | bytes accessed | tf_op | source)
XLA Modules:
  0.0 1428.4 jit_solution(5971478277093336269)
XLA Ops:
  12.0 6.6 reduce_sum.36
  20.3 27.3 %all-reduce = (f32[16]{0:T(128)S(1)}, f32[128]{0:T(128)S(1)}) all-reduce(f32[16]{0:T(128)S(1)} %reduce_sum.37, f32[128]{0:T(128)S(1)} %reduce_sum.36), channel_id=1, replica_groups=mesh['tm'=8,'chan'=4] {'tm'}, use_global_device_ids=true, to_apply=%region_5.6 | all-reduce | flops 144 | bytes 1152 | tf_op jit(solution)/shard_map/psum | solution.py:74
  47.8 19.1 %maximum_maximum_fusion = f32[144,36864]{1,0:T(8,128)} fusion(f32[16,4096]{1,0:T(8,128)S(1)} %collective-permute-done.1, f32[16,32768]{1,0:T(8,128)S(1)} %copy-done.3, f32[128,4096]{1,0:T(8,128)} %collective-permute-done, f32[128,32768]{1,0:T(8,128)} %param.4), kind=kLoop, calls=%fused_computation.82 | loop fusion | flops 15925248 | bytes 42467328 | tf_op jit(solution)/shard_map/concatenate | solution.py:99
  67.0 23.5 %reshape.135 = f32[144,9,4096]{2,1,0:T(8,128)} reshape(f32[144,36864]{1,0:T(8,128)} %maximum_maximum_fusion) | data formatting | bytes 42467328 | tf_op jit(solution)/shard_map/reshape | solution.py:66
  90.5 32.4 %fusion.86 = (f32[144,8,4096]{2,1,0:T(8,128)}, f32[144,8,4096]{2,1,0:T(8,128)}) fusion(f32[144,9,4096]{2,1,0:T(8,128)} %reshape.135), kind=kLoop, calls=%fused_computation.107 | loop fusion | bytes 75497472 | tf_op jit(solution)/shard_map/slice | solution.py:67
  122.9 24.7 %maximum_multiply_fusion = f32[18,64,8192]{2,1,0:T(8,128)} fusion(f32[18,64,4096]{2,1,0:T(8,128)} %bitcast.105, f32[18,64,4096]{2,1,0:T(8,128)} %bitcast.104, f32[8192]{0:T(1024)S(1)} %multiply_subtract_fusion.3), kind=kLoop, calls=%fused_computation.80 | loop fusion | flops 18874368 | bytes 75530240 | tf_op jit(solution)/shard_map/mul | solution.py:70
  147.6 768.6 %while.15 = (s32[]{:T(128)}, f32[18,64,4096]{2,1,0:T(8,128)}, bf16[18,64,4096]{2,1,0:T(8,128)(2,1)}, f32[18,64,8192]{2,1,0:T(8,128)}, s32[]{:T(128)}) while((s32[]{:T(128)}, f32[18,64,4096]{2,1,0:T(8,128)}, bf16[18,64,4096]{2,1,0:T(8,128)(2,1)}, f32[18,64,8192]{2,1,0:T(8,128)}, s32[]{:T(128)}) %tuple.35), condition=%wide.region_1.0_spmd, body=%wide.region_0.0_spmd.sunk | while | flops 2425782272 | bytes 54330460 | solution.py:60
  170.3 7.8 fusion.123
  178.1 9.2 add_bitcast_fusion.2
  212.9 7.8 fusion.123
  220.7 9.2 add_bitcast_fusion.2
  255.6 7.8 fusion.123
  263.4 9.2 add_bitcast_fusion.2
  298.3 7.8 fusion.123
  306.0 9.2 add_bitcast_fusion.2
  341.0 7.8 fusion.123
  348.8 9.2 add_bitcast_fusion.2
  373.8 6.3 subtract_bitcast_fusion.2
  383.6 7.8 fusion.123
  391.4 9.2 add_bitcast_fusion.2
  426.3 7.8 fusion.123
  434.1 9.2 add_bitcast_fusion.2
  468.9 7.8 fusion.123
  476.7 9.2 add_bitcast_fusion.2
  511.6 7.8 fusion.123
  519.4 9.2 add_bitcast_fusion.2
  554.2 7.8 fusion.123
  562.0 9.2 add_bitcast_fusion.2
  596.9 7.8 fusion.123
  604.7 9.2 add_bitcast_fusion.2
  639.6 7.8 fusion.123
  647.4 9.2 add_bitcast_fusion.2
  682.2 7.8 fusion.123
  690.0 9.2 add_bitcast_fusion.2
  715.1 6.3 subtract_bitcast_fusion.2
  724.9 7.8 fusion.123
  732.7 9.2 add_bitcast_fusion.2
  767.5 7.8 fusion.123
  775.3 9.2 add_bitcast_fusion.2
  810.3 7.8 fusion.123
  818.0 9.2 add_bitcast_fusion.2
  843.2 6.3 subtract_bitcast_fusion.2
  853.0 7.8 fusion.123
  860.8 9.2 add_bitcast_fusion.2
  895.7 7.8 fusion.123
  903.5 9.2 add_bitcast_fusion.2
  916.2 8.4 add_convert_fusion
  928.3 13.7 copy.33
  942.1 19.6 %reshape.143 = bf16[8,2,65536]{2,1,0:T(2,128)(2,1)} reshape(bf16[4096,2,8,16]{3,2,1,0:T(8,128)(2,1)} %bitcast.106) | data formatting | bytes 4194304
  966.8 14.8 %pad_maximum_fusion = bf16[2,128,8,4096]{3,2,1,0:T(8,128)(2,1)} fusion(bf16[1,144,8,4096]{3,2,1,0:T(8,128)(2,1)} %bitcast.110, bf16[1,144,8,4096]{3,2,1,0:T(8,128)(2,1)} %copy-done.1), kind=kLoop, calls=%fused_computation.84 | loop fusion | flops 8388608 | bytes 35651584 | tf_op jit(solution)/shard_map/stack | solution.py:118
  981.6 24.1 %copy.37 = bf16[2,128,8,4096]{1,2,0,3:T(8,128)(2,1)} copy(bf16[2,128,8,4096]{3,2,1,0:T(8,128)(2,1)} %pad_maximum_fusion) | data formatting | bytes 33554432 | tf_op jit(solution)/shard_map/slice | solution.py:120
  1011.4 13.2 reshape.144
  1024.7 16.0 %copy.34 = bf16[2,16,8,8,512]{4,1,3,2,0:T(8,128)(2,1)S(1)} copy(bf16[2,16,8,8,512]{1,3,0,4,2:T(8,128)(2,1)} %bitcast.107) | data formatting | bytes 4194304 | tf_op jit(solution)/shard_map/all_to_all | solution.py:124
  1042.2 149.3 %all-gather.3.cloned.1.call-done = bf16[8,16,63,512]{3,1,2,0:T(8,128)(2,1)} async-done(((bf16[2,16,63,512]{3,1,2,0:T(8,128)(2,1)}), bf16[8,16,63,512]{3,1,2,0:T(8,128)(2,1)}) %all-gather.3.cloned.1.call-update) | async-done | bytes 8257552 | tf_op jit(solution)/shard_map/all_gather | solution.py:14
  1197.5 15.3 %copy.35 = bf16[1,4,16,63,512]{3,2,1,4,0:T(8,128)(2,1)} copy(bf16[1,4,16,63,512]{4,2,3,0,1:T(8,128)(2,1)} %get-tuple-element.101) | data formatting | bytes 8257536 | tf_op jit(solution)/shard_map/slice | solution.py:80
  1212.9 15.4 %copy.36 = bf16[1,4,16,63,512]{3,2,1,4,0:T(8,128)(2,1)} copy(bf16[1,4,16,63,512]{4,2,3,0,1:T(8,128)(2,1)} %get-tuple-element.102) | data formatting | bytes 8257536 | tf_op jit(solution)/shard_map/slice | solution.py:80
  1233.7 25.2 %copy.39 = bf16[2,128,8,8,512]{4,3,2,1,0:T(8,128)(2,1)} copy(bf16[2,128,8,8,512]{1,3,0,4,2:T(8,128)(2,1)} %bitcast.22) | data formatting | bytes 33554432 | tf_op jit(solution)/shard_map/all_to_all | solution.py:123
  1258.9 13.6 fusion.87
  1279.4 26.8 %copy.46 = bf16[1,128,63,512]{2,1,3,0:T(8,128)(2,1)} copy(bf16[1,128,63,512]{3,2,1,0:T(8,128)(2,1)} %get-tuple-element.99) | data formatting | bytes 16515072
  1306.2 26.7 %copy.47 = bf16[1,128,63,512]{2,1,3,0:T(8,128)(2,1)} copy(bf16[1,128,63,512]{3,2,1,0:T(8,128)(2,1)} %get-tuple-element.100) | data formatting | bytes 16515072
  1332.8 14.3 %bitcast_negate_fusion = bf16[128,63,512]{1,0,2:T(8,128)(2,1)} fusion(bf16[1,128,63,512]{2,1,3,0:T(8,128)(2,1)} %copy.46), kind=kLoop, calls=%fused_computation.106 | loop fusion | flops 4128768 | bytes 16515072 | tf_op jit(solution)/shard_map/neg | solution.py:79
  1347.4 26.9 %fusion.74 = f32[512,64,128]{2,1,0:T(8,128)} fusion(bf16[128,63,512]{1,0,2:T(8,128)(2,1)} %bitcast.108, bf16[128,63,512]{1,0,2:T(8,128)(2,1)} %bitcast.103, bf16[64,63,512]{1,0,2:T(8,128)(2,1)} %bitcast.114, bf16[64,63,512]{1,0,2:T(8,128)(2,1)} %bitcast.112), kind=kOutput, calls=%fused_computation.85 | convolution fusion | flops 1106509824 | bytes 41549824 | tf_op jit(solution)/shard_map/csf,wsf->cwf/dot_general | solution.py:81
  1374.3 29.6 %bitcast_divide_fusion = f32[128,64,512]{0,1,2:T(8,128)} fusion(f32[512,64,128]{2,1,0:T(8,128)} %fusion.74, bf16[128,63,512]{1,0,2:T(8,128)(2,1)} %bitcast_negate_fusion, bf16[128,63,512]{1,0,2:T(8,128)(2,1)} %bitcast.109, f32[64,512]{0,1:T(8,128)S(1)} %copy.43, f32[128,512]{0,1:T(8,128)S(1)} %copy.42, bf16[64,63,512]{1,0,2:T(8,128)(2,1)} %bitcast.115, ...), kind=kOutput, calls=%fused_computation.93 | convolution fusion | flops 1127481344 | bytes 58720256 | tf_op jit(solution)/shard_map/csf,wsf->cwf/dot_general | solution.py:84
  1403.9 17.5 %copy.44 = f32[128,64,512]{2,1,0:T(8,128)} copy(f32[128,64,512]{0,1,2:T(8,128)} %bitcast_divide_fusion) | data formatting | bytes 33554432 | tf_op jit(solution)/shard_map/div | solution.py:89
  (273 shorter events, 484.7 us)
Async XLA Ops:
  9.6 9.0 copy-start.3
  9.6 38.2 %collective-permute-start = (f32[128,4096]{1,0:T(8,128)}, f32[128,4096]{1,0:T(8,128)}, u32[]{:S(2)}, u32[]{:S(2)}) collective-permute-start(f32[128,4096]{1,0:T(8,128)} %slice.42), channel_id=1, source_target_pairs={{4,0},{8,4},{12,8},{16,12},{20,16},{24,20},{28,24},{5,1},{9,5},{13... | collective-permute-start | bytes 6291464 | tf_op jit(solution)/shard_map/ppermute | solution.py:21
  19.0 28.8 %collective-permute-start.1 = (f32[16,4096]{1,0:T(8,128)S(1)}, f32[16,4096]{1,0:T(8,128)S(1)}, u32[]{:S(2)}, u32[]{:S(2)}) collective-permute-start(f32[16,4096]{1,0:T(8,128)S(1)} %slice.43), channel_id=1, source_target_pairs={{4,0},{8,4},{12,8},{16,12},{20,16},{24,20},{28,24},{5,1},{9,5},{13... | collective-permute-start | bytes 786440 | tf_op jit(solution)/shard_map/ppermute | solution.py:21
  154.1 6.4 copy-start
  196.8 6.4 copy-start
  239.4 6.4 copy-start
  282.1 6.4 copy-start
  324.8 6.4 copy-start
  367.5 6.4 copy-start
  410.1 6.4 copy-start
  452.8 6.4 copy-start
  495.4 6.4 copy-start
  538.1 6.4 copy-start
  580.7 6.4 copy-start
  623.4 6.4 copy-start
  666.1 6.4 copy-start
  708.7 6.4 copy-start
  751.4 6.4 copy-start
  794.0 6.4 copy-start
  836.8 6.4 copy-start
  879.5 6.4 copy-start
  916.2 11.9 copy-start.2
  924.6 3.5 copy-start.1
  961.6 44.0 %all-to-all-start = ((bf16[8,2,65536]{2,1,0:T(2,128)(2,1)}), bf16[8,2,65536]{2,1,0:T(2,128)(2,1)S(1)}, u32[]{:S(2)}, u32[]{:S(2)}) async-start(bf16[8,2,65536]{2,1,0:T(2,128)(2,1)} %reshape.143), calls=%async_computation | async-start | bytes 4194304 | tf_op jit(solution)/shard_map/all_to_all | solution.py:124
  1005.7 228.1 %all-to-all-start.1 = ((bf16[2,128,8,4096]{1,2,0,3:T(8,128)(2,1)}), bf16[2,128,8,4096]{1,2,0,3:T(8,128)(2,1)}, u32[]{:S(2)}, u32[]{:S(2)}) async-start(bf16[2,128,8,4096]{1,2,0,3:T(8,128)(2,1)} %copy.37), calls=%async_computation.1 | async-start | bytes 33554432 | tf_op jit(solution)/shard_map/all_to_all | solution.py:123
  1011.4 180.1 %all-gather.3.cloned.1.call-start = ((), (), s32[]{:S(2)}) async-start(), calls=%async_computation.2 | async-start | bytes 10321920 | tf_op jit(solution)/shard_map/all_gather | solution.py:14
  1258.9 13.6 slice-start
  1258.9 13.6 slice-start.1
  1258.9 15.3 %slice-start.2 = ((s8[16777216]{0:T(1024)(128)(4,1)}), s8[4194304]{0:T(1024)(128)(4,1)S(1)}, s32[]{:S(2)}) async-start(s8[16777216]{0:T(1024)(128)(4,1)} %bitcast.100), calls=%async_computation.5 | async-start | bytes 8388608
  1258.9 16.5 %slice-start.3 = ((s8[16777216]{0:T(1024)(128)(4,1)}), s8[4194304]{0:T(1024)(128)(4,1)S(1)}, s32[]{:S(2)}) async-start(s8[16777216]{0:T(1024)(128)(4,1)} %bitcast.100), calls=%async_computation.6 | async-start | bytes 8388608
Sparse Core Ops, SparseCore 0:
  1042.3 149.1 all-gather.2
